TPU v7x, 32 devices: a whole 2x2x4 slice. The times are simulated.
32 devices in a mesh: ka: 4 (over y, x), ga: 8 (over z, core).
Axes of the slice: x: 2, y: 2, z: 4, core: 2. Of those that a mesh axis runs over, the one named last changes fastest.
Arguments:
- coeffs: bfloat16 [4, 1, 65536, 2, 512], P('ka', None, 'ga'), may hold values from -0.5 to 0.5
- counts: int32 [4, 1], replicated, may hold values from 32768 to 65536
- block_map: int32 [4, 1, 2048], replicated, may hold values from 0 to 2047, as said below
- wrap: int32 [4, 1, 2048], replicated, may hold values from 0 to 31
Outputs:
- margins: float32 [4, 512, 1, 2, 512], P('ka', 'ga')
Inputs may be any that keep to these rules, and one draw needn't show every extreme that they name: For each k-point and line, block_map is a permutation of the 2048 blocks. Counting G-shards as runs of 256 blocks, at most 33 blocks of one shard have their partner blocks in any one shard, and for each k-point and line some pair of shards reaches 33.
All inputs are finite; a program needn't handle non-finite values.
Results may differ from a plain program's by a relative error of at most 0.0003.
Values may be sent and summed in bfloat16 or wider, within the bound.
No kernel may reach another device: no remote copies, remote signals or barrier semaphores. Data moves between devices by JAX's collectives and lax.ppermute only.
A program may use at most 128 MiB of HBM per device.

v0:
```python
import jax
import jax.numpy as jnp
from jax import lax
from jax.sharding import PartitionSpec as P

BLK = 32


def from_behind(value, axis, steps):
    count = lax.axis_size(axis)
    pairs = [(source, (source + steps) % count) for source in range(count)]
    return lax.ppermute(value, axis, pairs)


def slot_table(dest, ranking, values, shard_count, capacity):
    shard_ids = jnp.arange(shard_count, dtype=jnp.int32)
    slot_ids = jnp.arange(capacity, dtype=jnp.int32)
    hit = (dest[:, :, None, None] == shard_ids[None, None, :, None]) & (
        ranking[:, :, None, None] == slot_ids[None, None, None, :]
    )
    return jnp.sum(jnp.where(hit, values[:, :, None, None], 0), axis=1)


def pick_rows(source, picks):
    return jax.vmap(lambda rows_in, index_in: jnp.take(rows_in, index_in, axis=0))(source, picks)


def local(coeffs, counts, block_map, wrap):
    held_k = coeffs[0]
    line_count, g_rows, _, band_count = held_k.shape
    shard_count = lax.axis_size("ga")
    per_shard = g_rows // BLK
    block_total = block_map.shape[-1]
    capacity = block_total // (shard_count * shard_count) + 1
    k_index = lax.axis_index("ka")
    g_index = lax.axis_index("ga")
    k_total = counts.shape[0]
    count_here = counts[k_index]
    count_next = counts[(k_index + 1) % k_total]
    block_src = block_map[k_index]
    wrap_src = wrap[k_index]
    lane_ids = jnp.arange(BLK, dtype=jnp.int32)
    block_mine = lax.dynamic_slice_in_dim(block_src, g_index * per_shard, per_shard, 1)
    wrap_mine = lax.dynamic_slice_in_dim(wrap_src, g_index * per_shard, per_shard, 1)
    lane_shift = (lane_ids[None, None, :] + wrap_mine[:, :, None]) % BLK
    src_rows = block_mine[:, :, None] * BLK + lane_shift
    own_rows = g_index * g_rows + jnp.arange(g_rows, dtype=jnp.int32).reshape(per_shard, BLK)
    usable = (own_rows[None] < count_here[:, None, None]) & (src_rows < count_next[:, None, None])
    usable = usable.reshape(line_count, g_rows)
    masked_k = jnp.where(usable[:, :, None, None], held_k, jnp.zeros((), held_k.dtype))
    source_dev = block_mine // per_shard
    same_dev = source_dev[:, :, None] == source_dev[:, None, :]
    earlier = jnp.arange(per_shard)[:, None] > jnp.arange(per_shard)[None, :]
    rank_mine = jnp.sum((same_dev & earlier[None]).astype(jnp.int32), axis=2)
    coming = from_behind(held_k, "ka", -1)
    blocks_held = masked_k.reshape(line_count, per_shard, BLK, 2, band_count)
    back_lanes = (lane_ids[None, None, :] - wrap_mine[:, :, None]) % BLK
    rotated = jax.vmap(jax.vmap(lambda rows_in, index_in: jnp.take(rows_in, index_in, axis=0)))(
        blocks_held, back_lanes
    )
    local_ids = jnp.arange(per_shard, dtype=jnp.int32)[None, :]
    send_table = slot_table(source_dev, rank_mine, local_ids, shard_count, capacity)
    outgoing = pick_rows(rotated, send_table.reshape(line_count, -1))
    outgoing = outgoing.reshape(line_count, shard_count, capacity * BLK, 2, band_count)
    incoming = lax.all_to_all(outgoing, "ga", split_axis=1, concat_axis=1, tiled=True)
    incoming = incoming.reshape(line_count, shard_count * capacity * BLK, 2, band_count)
    inverse = jax.vmap(
        lambda perm_in: jnp.zeros((block_total,), jnp.int32)
        .at[perm_in]
        .set(jnp.arange(block_total, dtype=jnp.int32))
    )(block_src)
    target_mine = lax.dynamic_slice_in_dim(inverse, g_index * per_shard, per_shard, 1)
    sender = target_mine // per_shard
    to_me = block_src // per_shard == g_index
    rank_to_me = (
        jnp.cumsum(to_me.reshape(line_count, shard_count, per_shard).astype(jnp.int32), axis=2) - 1
    ).reshape(line_count, block_total)
    rank_sent = jnp.take_along_axis(rank_to_me, target_mine, axis=1)
    row_index = (
        (sender * capacity + rank_sent)[:, :, None] * BLK + lane_ids[None, None, :]
    ).reshape(line_count, g_rows)
    left_side = pick_rows(incoming, row_index)
    rows_here = band_count // shard_count
    products = jnp.einsum("lgcm,lgdn->mlcdn", left_side, coming, preferred_element_type=jnp.float32)
    real_part = products[:, :, 0, 0] + products[:, :, 1, 1]
    imag_part = products[:, :, 0, 1] - products[:, :, 1, 0]
    summed = lax.psum(jnp.stack([real_part, imag_part], axis=2), "ga")
    result = lax.dynamic_slice_in_dim(summed, g_index * rows_here, rows_here, 0)
    return result[None]


def solution(mesh):
    placed = (P("ka", None, "ga", None, None), P(), P(), P())
    return jax.shard_map(
        local,
        mesh=mesh,
        in_specs=placed,
        out_specs=P("ka", "ga", None, None, None),
        check_vma=False,
    )
```

profile of v0, /device:TPU:0, one launch (start us, length us, event | category | flops | bytes accessed | tf_op | source)
XLA Modules:
  0.0 826.9 jit_solution(5665315744447065316)
XLA Ops:
  6.5 0.8 and_select_fusion
  7.3 0.2 convert_reduce_fusion
  7.5 0.7 select_reduce_fusion
  8.2 0.1 copy.45
  8.3 0.1 copy.43
  8.4 0.1 reshape.1041
  8.6 0.1 broadcast_in_dim.90
  8.7 0.1 broadcast_in_dim.91
  8.8 0.1 copy.44
  8.9 0.1 reshape.1065
  9.0 1.4 constant_dynamic-slice_fusion.1
  10.4 1.6 compare_and_fusion
  12.0 21.3 %broadcast_select_fusion.2 = bf16[1,256,32,2,512]{4,3,2,1,0:T(2,128)(2,1)} fusion(bf16[1,256,32,2,512]{4,3,2,1,0:T(2,128)(2,1)} %bitcast.68, pred[256,32]{1,0:T(8,128)(4,1)S(1)} %get-tuple-element.14), kind=kLoop, calls=%fused_computation.7 | loop fusion | flops 8388608 | bytes 33562624 | tf_op jit(solution)/shard_map/jit(_where)/select_n | solution.py:50
  33.4 99.0 %gather_fusion.1 = bf16[8192,2,512]{2,1,0:T(2,128)(2,1)} fusion(bf16[1,256,32,2,512]{4,3,2,1,0:T(2,128)(2,1)} %broadcast_select_fusion.2, s32[8192]{0:T(1024)S(1)} %reshape.1065), kind=kCustom, calls=%fused_computation.1 | custom fusion | bytes 33652736 | tf_op jit(solution)/shard_map/vmap(vmap(jit(_take)))/gather | solution.py:58
  132.4 21.7 %broadcast_select_fusion.3 = bf16[1,256,32,2,512]{4,3,2,1,0:T(2,128)(2,1)} fusion(bf16[1,256,32,2,512]{4,3,2,1,0:T(2,128)(2,1)} %bitcast.69, pred[256,32]{1,0:T(8,128)(4,1)S(1)} %get-tuple-element.13), kind=kLoop, calls=%fused_computation.8 | loop fusion | flops 8388608 | bytes 33562624 | tf_op jit(solution)/shard_map/vmap(vmap(jit(_take)))/select_n | solution.py:58
  154.0 47.2 %gather_fusion.2 = bf16[264,32,2,512]{3,2,1,0:T(2,128)(2,1)} fusion(bf16[1,256,32,2,512]{4,3,2,1,0:T(2,128)(2,1)} %broadcast_select_fusion.3, s32[264]{0:T(512)S(1)} %fusion.45), kind=kCustom, calls=%fused_computation.2 | custom fusion | bytes 34605120 | tf_op jit(solution)/shard_map/vmap(jit(_take))/gather | solution.py:25
  201.2 25.0 %broadcast_select_fusion = bf16[1,8,1056,2,512]{4,3,2,0,1:T(2,128)(2,1)} fusion(bf16[1,8,1056,2,512]{4,3,2,0,1:T(2,128)(2,1)} %bitcast.67, pred[8,1056]{1,0:T(8,128)(4,1)S(1)} %broadcast_in_dim.91), kind=kLoop, calls=%fused_computation.5 | loop fusion | flops 8650752 | bytes 34611456 | tf_op jit(solution)/shard_map/vmap(jit(_take))/select_n | solution.py:25
  226.2 6.4 all-to-all-start
  232.6 0.0 copy-start
  232.6 0.0 copy-start.1
  232.6 0.0 all-reduce.2.cloned.1.call-start
  232.7 15.8 %copy.58 = bf16[1,1,8192,2,512]{4,2,3,1,0:T(8,128)(2,1)} copy(bf16[1,1,8192,2,512]{4,3,2,1,0:T(2,128)(2,1)} %param.4) | data formatting | bytes 33554432 | tf_op args[0]
  248.5 3.4 collective-permute-start
  251.8 0.7 compare_select_fusion.5
  252.6 0.6 reduce-window.6
  253.2 0.2 slice_reduce_fusion
  253.4 0.0 copy-done
  253.4 0.1 fusion.35
  253.5 0.0 copy-done.1
  253.5 0.1 and_reduce_fusion
  253.7 8.2 scatter_custom_fusion
  261.9 0.1 dynamic-slice.4
  262.0 0.1 copy.42
  262.1 0.1 broadcast.781
  262.2 1.7 gather_fusion
  263.9 0.1 add.349
  264.0 0.1 add.375
  264.1 0.1 add.350
  264.3 0.1 add.377
  264.4 0.1 add.352
  264.5 0.1 compare_select_fusion.1
  264.6 0.1 fusion.25
  264.7 343.0 %all-to-all-done = bf16[1,8,1056,2,512]{4,3,2,0,1:T(2,128)(2,1)} async-done(((bf16[1,8,1056,2,512]{4,3,2,0,1:T(2,128)(2,1)}), bf16[1,8,1056,2,512]{4,3,2,0,1:T(2,128)(2,1)}, u32[]{:S(2)}, u32[]{:S(2)}) %all-to-all-start) | async-done | bytes 17301536 | tf_op jit(solution)/shard_map/all_to_all | solution.py:65
  607.7 91.4 %gather_fusion.3 = bf16[8192,2,512]{2,1,0:T(2,128)(2,1)} fusion(bf16[1,8448,2,512]{3,2,1,0:T(2,128)(2,1)} %bitcast.20, s32[8192]{0:T(1024)S(1)} %bitcast.65), kind=kCustom, calls=%fused_computation.3 | custom fusion | bytes 33619968 | tf_op jit(solution)/shard_map/vmap(jit(_take))/gather | solution.py:25
  699.2 31.5 %fusion.3 = bf16[8192,2,512,1]{2,1,0,3:T(2,128)(2,1)S(1)} fusion(bf16[8192,2,512]{2,1,0:T(2,128)(2,1)} %gather_fusion.3, pred[8192]{0:T(1024)(128)(4,1)S(1)} %compare_and_fusion.1), kind=kLoop, calls=%fused_computation.13 | loop fusion | flops 8388608 | bytes 33562624 | tf_op jit(solution)/shard_map/vmap(jit(_take))/select_n | solution.py:25
  730.7 0.0 collective-permute-done
  730.7 20.7 %fusion.4 = f32[512,1,2,2,512]{4,0,3,2,1:T(8,128)S(1)} fusion(bf16[1,8192,2,512]{3,1,2,0:T(8,128)(2,1)} %collective-permute-done, bf16[8192,2,512,1]{2,1,0,3:T(2,128)(2,1)S(1)} %fusion.3), kind=kOutput, calls=%fused_computation.14 | convolution fusion | flops 17179869184 | bytes 37748736 | tf_op jit(solution)/shard_map/lgcm,lgdn->mlcdn/dot_general | solution.py:84
  751.4 0.5 fusion.10
  751.9 1.5 pad_maximum_fusion
  753.4 0.0 all-reduce.2.cloned.1.call-update
  753.4 64.8 %all-reduce.2.cloned.1.call-done = f32[512,1,2,512]{3,0,2,1:T(8,128)} async-done(((f32[512,1,2,512]{3,0,2,1:T(8,128)}), f32[512,1,2,512]{3,0,2,1:T(8,128)}) %all-reduce.2.cloned.1.call-update) | async-done | bytes 2097168 | tf_op jit(solution)/shard_map/psum | solution.py:87
  818.2 1.0 dynamic-slice_bitcast_fusion
  819.1 0.9 copy.48
  (26 shorter events, 0.3 us)
Async XLA Ops:
  226.2 381.5 %all-to-all-start = ((bf16[1,8,1056,2,512]{4,3,2,0,1:T(2,128)(2,1)}), bf16[1,8,1056,2,512]{4,3,2,0,1:T(2,128)(2,1)}, u32[]{:S(2)}, u32[]{:S(2)}) async-start(bf16[1,8,1056,2,512]{4,3,2,0,1:T(2,128)(2,1)} %broadcast_select_fusion), calls=%async_computation | async-start | bytes 34603008 | tf_op jit(solution)/shard_map/all_to_all | solution.py:65
  232.6 20.8 %copy-start = (s32[2]{0:T(128)S(1)}, s32[2]{0:T(128)}, u32[]{:S(2)}) copy-start(s32[2]{0:T(128)} %constant.184) | copy-start | bytes 28
  232.6 20.9 %copy-start.1 = (s32[2]{0:T(128)S(1)}, s32[2]{0:T(128)}, u32[]{:S(2)}) copy-start(s32[2]{0:T(128)} %constant.187) | copy-start | bytes 28
  232.6 585.6 %all-reduce.2.cloned.1.call-start = ((), (), s32[]{:S(2)}) async-start(), calls=%async_computation.1 | async-start | bytes 4194304 | tf_op jit(solution)/shard_map/psum | solution.py:87
  248.5 482.2 %collective-permute-start = (bf16[1,8192,2,512]{3,1,2,0:T(8,128)(2,1)}, bf16[1,8192,2,512]{3,1,2,0:T(8,128)(2,1)}, u32[]{:S(2)}, u32[]{:S(2)}) collective-permute-start(bf16[1,8192,2,512]{3,1,2,0:T(8,128)(2,1)} %bitcast.63), channel_id=1, source_target_pairs={{0,24},{8,0},{16,8},{24,16},{1,25},{9,1},{17,9},{25,17},{2,26},{10... | collective-permute-start | bytes 50331656 | tf_op jit(solution)/shard_map/ppermute | solution.py:12
Sparse Core Ops, SparseCore 0:
  753.5 64.6 all-reduce.1
where the time goes:
time: 827 us
  waiting for transfers between devices  408 us (49%)
  local copies, waits for them, and re-layouts  268 us (32%)
  other arithmetic  107 us (13%)
  matrix products  20.7 us (3%)
  between operations  13.7 us (2%)
  starting transfers between devices  9.76 us (1%)
    all_to_all x1, waiting for transfers between devices, local(): lax.all_to_all(outgoing, 'ga', split_axis=1, concat_axis=1, tiled=True)  343 us
    gather x4, local copies, waits for them, and re-layouts, pick_rows(): jnp.take(rows_in, index_in, axis=0)  139 us
    gather x3, local copies, waits for them, and re-layouts, local(): jnp.take(rows_in, index_in, axis=0)  99.2 us
    psum x1, waiting for transfers between devices, local(): summed = lax.psum(jnp.stack([real_part, imag_part], axis=2), 'ga')  64.8 us
    select_n x4, other arithmetic, pick_rows(): jnp.take(rows_in, index_in, axis=0)  56.6 us
    unnamed x9, local copies, waits for them, and re-layouts  24.2 us
    select_n x2, other arithmetic, local(): jnp.take(rows_in, index_in, axis=0)  21.7 us
    select_n x1, other arithmetic, local(): jnp.where(usable[:, :, None, None], held_k, jnp.zeros((), held_k.dtype))  21.3 us
  transfers between devices with their start and end apart: 3, of which 2 were waited for; matrix products, arithmetic and copies ran while one was open for 18% of the time, Pallas kernels for 0%

commit v1 on v0

--- a/solution.py
+++ b/solution.py
@@ -84,7 +84,7 @@
     products = jnp.einsum("lgcm,lgdn->mlcdn", left_side, coming, preferred_element_type=jnp.float32)
     real_part = products[:, :, 0, 0] + products[:, :, 1, 1]
     imag_part = products[:, :, 0, 1] - products[:, :, 1, 0]
-    summed = lax.psum(jnp.stack([real_part, imag_part], axis=2), "ga")
+    summed = jnp.sum(lax.all_gather(jnp.stack([real_part, imag_part], axis=2), "ga"), axis=0)
     result = lax.dynamic_slice_in_dim(summed, g_index * rows_here, rows_here, 0)
     return result[None]
 

time: 827 us -> 921 us (1.11)
  waiting for transfers between devices: 408 us -> 494 us
    all_gather x0 -> x1, waiting for transfers between devices: none -> 151 us  [local(): lax.all_gather(jnp.stack([real_part, imag_part], axis=2), 'ga')]
    psum x1 -> x0, waiting for transfers between devices: 64.8 us -> none  [local(): summed = lax.psum(jnp.stack([real_part, imag_part], axis=2), 'ga')]
  transfers between devices with their start and end apart: 3 -> 3, of which waited for: 2 -> 2; matrix products, arithmetic and copies ran while one was open for 18% -> 16% of each run, Pallas kernels for 0% -> 0%
where the time goes in v1:
time: 921 us; the launch traced here: 920 us
  waiting for transfers between devices  494 us (54%)
  local copies, waits for them, and re-layouts  267 us (29%)
  other arithmetic  115 us (12%)
  matrix products  20.7 us (2%)
  between operations  13.7 us (1%)
  starting transfers between devices  9.76 us (1%)
    all_to_all x1, waiting for transfers between devices, local(): lax.all_to_all(outgoing, 'ga', split_axis=1, concat_axis=1, tiled=True)  343 us
    all_gather x1, waiting for transfers between devices, local(): lax.all_gather(jnp.stack([real_part, imag_part], axis=2), 'ga')  151 us
    gather x4, local copies, waits for them, and re-layouts, pick_rows(): jnp.take(rows_in, index_in, axis=0)  139 us
    gather x3, local copies, waits for them, and re-layouts, local(): jnp.take(rows_in, index_in, axis=0)  99.2 us
    select_n x4, other arithmetic, pick_rows(): jnp.take(rows_in, index_in, axis=0)  56.6 us
    unnamed x9, local copies, waits for them, and re-layouts  24.2 us
    select_n x2, other arithmetic, local(): jnp.take(rows_in, index_in, axis=0)  21.7 us
    select_n x1, other arithmetic, local(): jnp.where(usable[:, :, None, None], held_k, jnp.zeros((), held_k.dtype))  21.3 us
  transfers between devices with their start and end apart: 3, of which 2 were waited for; matrix products, arithmetic and copies ran while one was open for 16% of the time, Pallas kernels for 0%

profile of v1, /device:TPU:0, one launch (start us, length us, event | category | flops | bytes accessed | tf_op | source)
XLA Modules:
  0.0 920.1 jit_solution(1610816842435526989)
XLA Ops:
  6.5 0.8 and_select_fusion
  7.3 0.2 convert_reduce_fusion
  7.5 0.7 select_reduce_fusion
  8.2 0.1 copy.50
  8.3 0.1 copy.48
  8.4 0.1 reshape.1044
  8.6 0.1 broadcast_in_dim.90
  8.7 0.1 broadcast_in_dim.91
  8.8 0.1 copy.49
  8.9 0.1 reshape.1068
  9.0 1.4 constant_dynamic-slice_fusion.1
  10.4 1.6 compare_and_fusion
  12.0 21.3 %broadcast_select_fusion.2 = bf16[1,256,32,2,512]{4,3,2,1,0:T(2,128)(2,1)} fusion(bf16[1,256,32,2,512]{4,3,2,1,0:T(2,128)(2,1)} %bitcast.69, pred[256,32]{1,0:T(8,128)(4,1)S(1)} %get-tuple-element.14), kind=kLoop, calls=%fused_computation.7 | loop fusion | flops 8388608 | bytes 33562624 | tf_op jit(solution)/shard_map/jit(_where)/select_n | solution.py:50
  33.4 99.0 %gather_fusion.1 = bf16[8192,2,512]{2,1,0:T(2,128)(2,1)} fusion(bf16[1,256,32,2,512]{4,3,2,1,0:T(2,128)(2,1)} %broadcast_select_fusion.2, s32[8192]{0:T(1024)S(1)} %reshape.1068), kind=kCustom, calls=%fused_computation.1 | custom fusion | bytes 33652736 | tf_op jit(solution)/shard_map/vmap(vmap(jit(_take)))/gather | solution.py:58
  132.4 21.7 %broadcast_select_fusion.3 = bf16[1,256,32,2,512]{4,3,2,1,0:T(2,128)(2,1)} fusion(bf16[1,256,32,2,512]{4,3,2,1,0:T(2,128)(2,1)} %bitcast.70, pred[256,32]{1,0:T(8,128)(4,1)S(1)} %get-tuple-element.13), kind=kLoop, calls=%fused_computation.8 | loop fusion | flops 8388608 | bytes 33562624 | tf_op jit(solution)/shard_map/vmap(vmap(jit(_take)))/select_n | solution.py:58
  154.0 47.2 %gather_fusion.2 = bf16[264,32,2,512]{3,2,1,0:T(2,128)(2,1)} fusion(bf16[1,256,32,2,512]{4,3,2,1,0:T(2,128)(2,1)} %broadcast_select_fusion.3, s32[264]{0:T(512)S(1)} %fusion.45), kind=kCustom, calls=%fused_computation.2 | custom fusion | bytes 34605120 | tf_op jit(solution)/shard_map/vmap(jit(_take))/gather | solution.py:25
  201.2 25.0 %broadcast_select_fusion = bf16[1,8,1056,2,512]{4,3,2,0,1:T(2,128)(2,1)} fusion(bf16[1,8,1056,2,512]{4,3,2,0,1:T(2,128)(2,1)} %bitcast.68, pred[8,1056]{1,0:T(8,128)(4,1)S(1)} %broadcast_in_dim.91), kind=kLoop, calls=%fused_computation.5 | loop fusion | flops 8650752 | bytes 34611456 | tf_op jit(solution)/shard_map/vmap(jit(_take))/select_n | solution.py:25
  226.2 6.4 all-to-all-start
  232.6 0.0 copy-start
  232.6 0.0 copy-start.1
  232.6 0.0 all-gather.3.cloned.1.call-start
  232.7 15.8 %copy.63 = bf16[1,1,8192,2,512]{4,2,3,1,0:T(8,128)(2,1)} copy(bf16[1,1,8192,2,512]{4,3,2,1,0:T(2,128)(2,1)} %param.4) | data formatting | bytes 33554432 | tf_op args[0]
  248.5 3.4 collective-permute-start
  251.8 0.7 compare_select_fusion.5
  252.6 0.6 reduce-window.6
  253.2 0.2 slice_reduce_fusion
  253.4 0.0 copy-done
  253.4 0.1 fusion.35
  253.5 0.0 copy-done.1
  253.5 0.1 and_reduce_fusion
  253.7 8.2 scatter_custom_fusion
  261.9 0.1 dynamic-slice.8
  262.0 0.1 copy.47
  262.1 0.1 broadcast.781
  262.2 1.7 gather_fusion
  263.9 0.1 add.347
  264.0 0.1 add.373
  264.1 0.1 add.348
  264.3 0.1 add.375
  264.4 0.1 add.350
  264.5 0.1 compare_select_fusion.1
  264.6 0.1 fusion.25
  264.7 343.0 %all-to-all-done = bf16[1,8,1056,2,512]{4,3,2,0,1:T(2,128)(2,1)} async-done(((bf16[1,8,1056,2,512]{4,3,2,0,1:T(2,128)(2,1)}), bf16[1,8,1056,2,512]{4,3,2,0,1:T(2,128)(2,1)}, u32[]{:S(2)}, u32[]{:S(2)}) %all-to-all-start) | async-done | bytes 17301536 | tf_op jit(solution)/shard_map/all_to_all | solution.py:65
  607.7 91.4 %gather_fusion.3 = bf16[8192,2,512]{2,1,0:T(2,128)(2,1)} fusion(bf16[1,8448,2,512]{3,2,1,0:T(2,128)(2,1)} %bitcast.20, s32[8192]{0:T(1024)S(1)} %bitcast.66), kind=kCustom, calls=%fused_computation.3 | custom fusion | bytes 33619968 | tf_op jit(solution)/shard_map/vmap(jit(_take))/gather | solution.py:25
  699.2 31.5 %fusion.3 = bf16[8192,2,512,1]{2,1,0,3:T(2,128)(2,1)S(1)} fusion(bf16[8192,2,512]{2,1,0:T(2,128)(2,1)} %gather_fusion.3, pred[8192]{0:T(1024)(128)(4,1)S(1)} %compare_and_fusion.1), kind=kLoop, calls=%fused_computation.13 | loop fusion | flops 8388608 | bytes 33562624 | tf_op jit(solution)/shard_map/vmap(jit(_take))/select_n | solution.py:25
  730.7 0.0 collective-permute-done
  730.7 20.7 %fusion.4 = f32[512,1,2,2,512]{4,0,3,2,1:T(8,128)S(1)} fusion(bf16[1,8192,2,512]{3,1,2,0:T(8,128)(2,1)} %collective-permute-done, bf16[8192,2,512,1]{2,1,0,3:T(2,128)(2,1)S(1)} %fusion.3), kind=kOutput, calls=%fused_computation.14 | convolution fusion | flops 17179869184 | bytes 37748736 | tf_op jit(solution)/shard_map/lgcm,lgdn->mlcdn/dot_general | solution.py:84
  751.4 0.5 fusion.10
  751.9 1.5 pad_maximum_fusion
  753.4 0.0 all-gather.3.cloned.1.call-update
  753.4 150.8 %all-gather.3.cloned.1.call-done = f32[4096,1,2,512]{3,0,2,1:T(8,128)} async-done(((f32[512,1,2,512]{3,0,2,1:T(8,128)}), f32[4096,1,2,512]{3,0,2,1:T(8,128)}) %all-gather.3.cloned.1.call-update) | async-done | bytes 16777232 | tf_op jit(solution)/shard_map/all_gather | solution.py:87
  904.2 8.1 reduce.7
  912.3 0.9 copy.53
  (27 shorter events, 0.4 us)
Async XLA Ops:
  226.2 381.5 %all-to-all-start = ((bf16[1,8,1056,2,512]{4,3,2,0,1:T(2,128)(2,1)}), bf16[1,8,1056,2,512]{4,3,2,0,1:T(2,128)(2,1)}, u32[]{:S(2)}, u32[]{:S(2)}) async-start(bf16[1,8,1056,2,512]{4,3,2,0,1:T(2,128)(2,1)} %broadcast_select_fusion), calls=%async_computation | async-start | bytes 34603008 | tf_op jit(solution)/shard_map/all_to_all | solution.py:65
  232.6 20.8 %copy-start = (s32[2]{0:T(128)S(1)}, s32[2]{0:T(128)}, u32[]{:S(2)}) copy-start(s32[2]{0:T(128)} %constant.186) | copy-start | bytes 28
  232.6 20.9 %copy-start.1 = (s32[2]{0:T(128)S(1)}, s32[2]{0:T(128)}, u32[]{:S(2)}) copy-start(s32[2]{0:T(128)} %constant.189) | copy-start | bytes 28
  232.6 671.6 %all-gather.3.cloned.1.call-start = ((), (), s32[]{:S(2)}) async-start(), calls=%async_computation.1 | async-start | bytes 18874368 | tf_op jit(solution)/shard_map/all_gather | solution.py:87
  248.5 482.2 %collective-permute-start = (bf16[1,8192,2,512]{3,1,2,0:T(8,128)(2,1)}, bf16[1,8192,2,512]{3,1,2,0:T(8,128)(2,1)}, u32[]{:S(2)}, u32[]{:S(2)}) collective-permute-start(bf16[1,8192,2,512]{3,1,2,0:T(8,128)(2,1)} %bitcast.64), channel_id=1, source_target_pairs={{0,24},{8,0},{16,8},{24,16},{1,25},{9,1},{17,9},{25,17},{2,26},{10... | collective-permute-start | bytes 50331656 | tf_op jit(solution)/shard_map/ppermute | solution.py:12
Sparse Core Ops, SparseCore 0:
  753.6 150.6 all-gather.2
